TPU v7x, 32 devices: a whole 2x2x4 slice. The times are simulated.
32 devices in a mesh: dp: 4 (over y, core), fsdp: 8 (over z, x).
Axes of the slice: x: 2, y: 2, z: 4, core: 2. Of those that a mesh axis runs over, the one named last changes fastest.
Arguments:
- images: bfloat16 [192, 784, 320], P(('dp', 'fsdp')), may hold values from -50 to 50
- counts: int32 [32], P(('dp', 'fsdp')), may hold values from 1 to 6, 96 in all
- cotangent: bfloat16 [192, 784, 320], P(('dp', 'fsdp')), may hold values from -6 to 6
- master: float32 [1658880], P(('dp', 'fsdp')), may hold values from -4 to 4
- first_moment: float32 [1658880], P(('dp', 'fsdp')), may hold values from -219.47428 to 219.47428
- second_moment: float32 [1658880], P(('dp', 'fsdp')), may hold values from 737.5872 to 12268.032, as said below
- average: float32 [1658880], P(('dp', 'fsdp')), may hold values from -4 to 4
Outputs:
- grads: float32 [1658880], P(('dp', 'fsdp'))
- new_first: float32 [1658880], P(('dp', 'fsdp'))
- new_second: float32 [1658880], P(('dp', 'fsdp'))
- new_master: float32 [1658880], P(('dp', 'fsdp'))
- new_average: float32 [1658880], P(('dp', 'fsdp'))
- new_copy: bfloat16 [1658880], P(('dp', 'fsdp'))
- output_images: bfloat16 [192, 784, 320], P(('dp', 'fsdp'))
- grad_images: bfloat16 [192, 784, 320], P(('dp', 'fsdp'))
Inputs may be any that keep to these rules, and one draw needn't show every extreme that they name: counts sum to 96; at least one device holds exactly 6. `second_moment`: positive.
All inputs are finite; a program needn't handle non-finite values.
Results may differ from a plain program's by a relative error of at most 0.013.
The roundings to bfloat16 on the way count: a program that leaves them out, or rounds other values in their place, can miss the bound.
Values may be sent and summed in bfloat16 or wider, within the bound.
A program may use at most 128 MiB of HBM per device.

v0:
```python
import math

import jax
import jax.numpy as jnp
from jax import lax
from jax.experimental import pallas as pl
from jax.experimental.pallas import tpu as pltpu
from jax.sharding import PartitionSpec as P

C = 320
HEADS = 5
HEADSZ = 64
HID = 1280
SIDE = 28
STEP = 3
HALF = 14
NTOK = 784
KEYS = 196


norm_eps = 1e-06
adam_eps = 1e-08
learn_rate = 0.02
weight_decay = 0.05
beta_first = 0.5
beta_second = 0.5
ema_keep = 0.9


def segments():
    return [
        ("norm_gain", (C,)),
        ("norm_bias", (C,)),
        ("query_weight", (C, C)),
        ("query_bias", (C,)),
        ("reduce_weight", (4 * C, C)),
        ("reduce_bias", (C,)),
        ("keys_gain", (C,)),
        ("keys_bias", (C,)),
        ("kv_weight", (C, 2 * C)),
        ("value_bias", (C,)),
        ("out_weight", (C, C)),
        ("out_bias", (C,)),
        ("mlp_gain", (C,)),
        ("mlp_bias", (C,)),
        ("up_weight", (C, HID)),
        ("up_bias", (HID,)),
        ("depth_weight", (9, HID)),
        ("depth_bias", (HID,)),
        ("down_weight", (HID, C)),
        ("down_bias", (C,)),
    ]


def unpack(flat_vector):
    pieces = {}
    offset = 0
    for seg_name, seg_shape in segments():
        seg_size = math.prod(seg_shape)
        pieces[seg_name] = flat_vector[offset : offset + seg_size].reshape(seg_shape)
        offset += seg_size
    return pieces


TOK = 1024
SLAB = 256
KEYC = 208
BLK = 256
NBLK = HID // BLK
F32 = jnp.float32
BF16 = jnp.bfloat16
ERFC_C = 0.35
ERFC_P = (
    0.1397766380054567,
    0.13686603367482672,
    0.1431944963239702,
    0.00881332607675965,
    0.2112475588897874,
    -0.18454519984085327,
    0.04464718332154041,
)
LOG2E = 1.4426950408889634
V_NG, V_NB, V_QB, V_RB, V_KG, V_KB, V_VB, V_OB, V_MG, V_MB, V_DB = range(11)


def dot_nn(left, right):
    return lax.dot_general(left, right, (((1,), (0,)), ((), ())), preferred_element_type=F32)


def dot_nt(left, right):
    return lax.dot_general(left, right, (((1,), (1,)), ((), ())), preferred_element_type=F32)


def fold(x):
    total = x[:, :128]
    for k in range(1, x.shape[1] // 128):
        total = total + x[:, 128 * k : 128 * (k + 1)]
    return total


def aligned(value, step):
    return pl.multiple_of(value, step)


def column(ref, row, lane):
    return ref[pl.ds(row, 8), :][:, lane : lane + 1]


def ln_stats(src, width):
    def first(i, acc):
        return acc + src[pl.ds(aligned(8 * i, 8), 8), :]

    acc = lax.fori_loop(0, C // 8, first, jnp.zeros((8, width), F32), unroll=4)
    mean = jnp.broadcast_to(jnp.sum(acc, 0, keepdims=True) * (1.0 / C), (8, width))

    def second(i, acc):
        d = src[pl.ds(aligned(8 * i, 8), 8), :] - mean
        return acc + d * d

    acc = lax.fori_loop(0, C // 8, second, jnp.zeros((8, width), F32), unroll=4)
    inv = lax.rsqrt(jnp.sum(acc, 0, keepdims=True) * (1.0 / C) + norm_eps)
    return mean, jnp.broadcast_to(inv, (8, width))


def ln_apply(src, dst, mean, inv, vt, gain_lane, bias_lane):
    def step(i, carry):
        row = aligned(16 * i, 16)
        parts = []
        for half in range(2):
            r = aligned(row + 8 * half, 8)
            u = (src[pl.ds(r, 8), :] - mean) * inv
            parts.append(u * column(vt, r, gain_lane) + column(vt, r, bias_lane))
        dst[pl.ds(row, 16), :] = jnp.concatenate(parts, 0).astype(BF16)
        return carry

    lax.fori_loop(0, C // 16, step, 0, unroll=2)


def norm_back(grad, src, mean, inv, vt, gain_lane, gv, gain_slot, bias_slot, emit):
    width = mean.shape[1]

    def first(i, carry):
        acc_one, acc_two = carry
        r = aligned(8 * i, 8)
        u = (src[pl.ds(r, 8), :] - mean) * inv
        d = grad[pl.ds(r, 8), :]
        du = d * u
        gain = column(vt, r, gain_lane)
        gv[gain_slot, pl.ds(r, 8), :] += fold(du)
        gv[bias_slot, pl.ds(r, 8), :] += fold(d)
        return acc_one + d * gain, acc_two + du * gain

    zero = jnp.zeros((8, width), F32)
    acc_one, acc_two = lax.fori_loop(0, C // 8, first, (zero, zero), unroll=2)
    m_one = jnp.broadcast_to(jnp.sum(acc_one, 0, keepdims=True) * (1.0 / C), (8, width))
    m_two = jnp.broadcast_to(jnp.sum(acc_two, 0, keepdims=True) * (1.0 / C), (8, width))

    def second(i, carry):
        row = aligned(16 * i, 16)
        parts = []
        for half in range(2):
            r = aligned(row + 8 * half, 8)
            u = (src[pl.ds(r, 8), :] - mean) * inv
            d = grad[pl.ds(r, 8), :] * column(vt, r, gain_lane)
            parts.append(inv * (d - m_one - u * m_two))
        emit(row, parts)
        return carry

    lax.fori_loop(0, C // 16, second, 0)


def shift_down(v, low):
    a, b = pltpu.roll(v[0], 16, 1), pltpu.roll(v[1], 16, 1)
    return [jnp.where(low, b, a), jnp.where(low, a, b)]


def shift_up(v, high):
    a, b = pltpu.roll(v[0], 112, 1), pltpu.roll(v[1], 112, 1)
    return [jnp.where(high, b, a), jnp.where(high, a, b)]


def side_views(e):
    views = {}
    for a in range(2):
        left = [pltpu.roll(v, 1, 1) for v in e[a, 1]]
        right = [pltpu.roll(v, 127, 1) for v in e[a, 0]]
        views[a, 0] = (left, e[a, 0], e[a, 1])
        views[a, 1] = (e[a, 0], e[a, 1], right)
    return views


def conv(views, taps, bias, low, high):
    def combo(a, b, row):
        out = []
        for h in range(2):
            t = views[a, b][0][h] * taps[row][0]
            t = t + views[a, b][1][h] * taps[row][1]
            out.append(t + views[a, b][2][h] * taps[row][2])
        return out

    result = {}
    for b in range(2):
        top = shift_down(combo(1, b, 0), low)
        mid, bot = combo(0, b, 1), combo(1, b, 2)
        result[0, b] = [top[h] + mid[h] + bot[h] for h in range(2)]
        top, mid = combo(0, b, 0), combo(1, b, 1)
        bot = shift_up(combo(0, b, 2), high)
        result[1, b] = [top[h] + mid[h] + bot[h] for h in range(2)]
        if bias is not None:
            for a in range(2):
                result[a, b] = [v + bias for v in result[a, b]]
    return result


def tap_grads(views, dd, low, high):
    sums = [[None] * 3 for _ in range(3)]
    for b in range(2):
        up = shift_up(dd[0, b], high)
        down = shift_down(dd[1, b], low)
        pairs = ((up, views[1, b], dd[1, b], views[0, b]),
                 (dd[0, b], views[0, b], dd[1, b], views[1, b]),
                 (dd[0, b], views[1, b], down, views[0, b]))
        for row in range(3):
            g_one, v_one, g_two, v_two = pairs[row]
            for col in range(3):
                t = sums[row][col]
                for h in range(2):
                    p = g_one[h] * v_one[col][h] + g_two[h] * v_two[col][h]
                    t = p if t is None else t + p
                sums[row][col] = t
    return sums


def gelu_parts(z):
    t = 1.0 / (1.0 + ERFC_C * jnp.abs(z))
    poly = ERFC_P[6]
    for k in range(5, -1, -1):
        poly = poly * t + ERFC_P[k]
    e = jnp.exp2(z * z * (-0.5 * LOG2E))
    q = poly * t * e
    phi = jnp.where(z < 0, q, 1.0 - q)
    return z * phi, phi + z * e * (1.0 / math.sqrt(2.0 * math.pi))


def image_kernel(
    n_ref, x_ref, ct_ref,
    wqt, wrt, wkvt, wot, wut, wdt, wq, wr, wkv, wo, wu, wd, vt, ht,
    out_ref, gin_ref, gwq_o, gwr_o, gwkv_o, gwo_o, gwu_o, gwd_o, gv_o, gh_o,
    gwq, gwr, gwkv, gwo, gwu, gwd, gv, gh,
    eye, sel, xf, xp, xt, dzt, hgt, qt, att, attb, mt, yt, acc, dgt, dbt, dmt, dqt,
    rt, nt, kvt, kvc, kc, vc, dsb, dkvc, e_s, du_s, u_s, de_s, stat, sem,
):
    slot = pl.program_id(0)
    live = n_ref[0]
    lanes = lax.broadcasted_iota(jnp.int32, (8, 128), 1)
    low, high = lanes < 16, lanes >= 112

    @pl.when(slot == 0)
    def _():
        for ref in (gwq, gwr, gwkv, gwo, gwu, gwd, gv, gh, xp):
            ref[...] = jnp.zeros(ref.shape, ref.dtype)
        r = lax.broadcasted_iota(jnp.int32, (C, C), 0)
        c = lax.broadcasted_iota(jnp.int32, (C, C), 1)
        eye[...] = (r == c).astype(F32).astype(BF16)
        r = lax.broadcasted_iota(jnp.int32, (KEYC, SLAB), 0)
        c = lax.broadcasted_iota(jnp.int32, (KEYC, SLAB), 1)
        i, j = c >> 4, c & 15
        hit = (r == i * HALF + j) & (i < HALF) & (j < HALF)
        sel[...] = hit.astype(F32).astype(BF16)

    def take(src, dst):
        def widen(k, carry):
            row = aligned(112 * k, 16)
            rows = src[0, pl.ds(row, 112), :].astype(F32)
            xf[0, pl.ds(row, 112), :] = rows[:, :128]
            xf[1, pl.ds(row, 112), :] = rows[:, 128:256]
            xf[2, pl.ds(row, 112), :64] = rows[:, 256:]
            return carry

        lax.fori_loop(0, 7, widen, 0)

        def split(i, carry):
            for a in range(2):
                for b in range(2):
                    at = pl.ds(aligned((2 * a + b) * SLAB + 16 * i, 16), HALF)
                    for t in range(3):
                        rows = xf.at[t][pl.ds(56 * i + 28 * a + b, HALF, stride=2), :]
                        xp[at, 128 * t : 128 * (t + 1)] = rows
            return carry

        lax.fori_loop(0, HALF, split, 0)
        for k in range(4):
            part = xp[SLAB * k : SLAB * (k + 1), :C].astype(BF16)
            dst[:, SLAB * k : SLAB * (k + 1)] = dot_nt(eye[...], part).astype(dst.dtype)

    def give(src, dst):
        for k in range(4):
            e_s[:, :C] = dot_nt(eye[:SLAB, :SLAB], src[:, SLAB * k : SLAB * (k + 1)])

            def spread(i, carry):
                at = pl.ds(aligned(16 * i, 16), HALF)
                for t in range(3):
                    rows = e_s[at, 128 * t : 128 * (t + 1)]
                    xf.at[t][pl.ds(56 * i + 28 * (k // 2) + (k % 2), HALF, stride=2), :] = rows
                return carry

            lax.fori_loop(0, HALF, spread, 0)

        def narrow(k, carry):
            row = aligned(112 * k, 16)
            dst[0, pl.ds(row, 112), :128] = xf[0, pl.ds(row, 112), :].astype(BF16)
            dst[0, pl.ds(row, 112), 128:256] = xf[1, pl.ds(row, 112), :].astype(BF16)
            dst[0, pl.ds(row, 112), 256:] = xf[2, pl.ds(row, 112), :64].astype(BF16)
            return carry

        lax.fori_loop(0, 7, narrow, 0)

    @pl.when(slot >= live)
    def _():
        out_ref[...] = jnp.zeros(out_ref.shape, BF16)
        gin_ref[...] = jnp.zeros(gin_ref.shape, BF16)

    @pl.when(slot < live)
    def _():
        take(x_ref, xt)
        take(ct_ref, dzt)
        mean, inv = ln_stats(xt, TOK)
        stat[0], stat[1] = mean, inv
        ln_apply(xt, hgt.at[0], mean, inv, vt, V_NG, V_NB)
        ht_ = hgt.at[0]
        qt[...] = (dot_nn(wqt[...], ht_[...]) + vt[:, V_QB : V_QB + 1]).astype(BF16)
        reduced = vt[:, V_RB : V_RB + 1]
        for k in range(4):
            reduced = reduced + dot_nn(wrt[k], ht_[:, SLAB * k : SLAB * (k + 1)])
        rt[...] = reduced
        kmean, kinv = ln_stats(rt, SLAB)
        stat[4, :, :SLAB], stat[5, :, :SLAB] = kmean, kinv
        ln_apply(rt, nt, kmean, kinv, vt, V_KG, V_KB)
        kvt[:C, :] = dot_nn(wkvt[:C, :], nt[...]).astype(BF16)
        kvt[C:, :] = (dot_nn(wkvt[C:, :], nt[...]) + vt[:, V_VB : V_VB + 1]).astype(BF16)
        kvc[...] = dot_nt(kvt[...], sel[...]).astype(BF16)

        def head_forward(h, carry):
            r = aligned(HEADSZ * h, HEADSZ)
            kc[h] = dot_nt(sel[...], kvt[pl.ds(r, HEADSZ), :]).astype(BF16)
            vc[h] = dot_nt(sel[...], kvt[pl.ds(aligned(C + r, HEADSZ), HEADSZ), :]).astype(BF16)
            att[h] = dot_nn(kc[h], qt[pl.ds(r, HEADSZ), :])

            def tile(t, carry):
                ls = pl.ds(aligned(128 * t, 128), 128)
                s = att[h, :, ls]
                rows = lax.broadcasted_iota(jnp.int32, (KEYC, 128), 0)
                s = jnp.where(rows < KEYS, s, -jnp.inf)
                top = jnp.max(s, 0, keepdims=True)
                p = jnp.exp2((s - top) * (LOG2E * HEADSZ**-0.5))
                p = p * (1.0 / jnp.sum(p, 0, keepdims=True))
                att[h, :, ls] = p
                attb[h, :, ls] = p.astype(BF16)
                return carry

            lax.fori_loop(0, TOK // 128, tile, 0)
            vt_h = kvc[pl.ds(aligned(C + r, HEADSZ), HEADSZ), :]
            mt[pl.ds(r, HEADSZ), :] = dot_nn(vt_h, attb[h]).astype(BF16)
            return carry

        lax.fori_loop(0, HEADS, head_forward, 0)
        yt[...] = xt[...] + (dot_nn(wot[...], mt[...]) + vt[:, V_OB : V_OB + 1])
        mean, inv = ln_stats(yt, TOK)
        stat[2], stat[3] = mean, inv
        ln_apply(yt, hgt.at[1], mean, inv, vt, V_MG, V_MB)
        gt = hgt.at[1]
        acc[...] = yt[...] + vt[:, V_DB : V_DB + 1]
        dgt[...] = jnp.zeros(dgt.shape, F32)
        lane16 = (lanes & 15) < HALF
        keep = (lane16, lane16 & (lanes < 96))

        def block(c, carry):
            e_s[...] = dot_nn(wut[c], gt[...])
            du_s[...] = dot_nn(wd[c], dzt[...])

            def group(i, carry):
                row = aligned(16 * i, 16)
                u_parts, de_parts = [], []
                for half in range(2):
                    r = aligned(row + 8 * half, 8)
                    chan = aligned(BLK * c + r, 8)
                    table = ht[pl.ds(chan, 8), :]
                    w = [jnp.broadcast_to(table[:, k : k + 1], (8, 128)) for k in range(11)]
                    taps = [w[0:3], w[3:6], w[6:9]]
                    flipped = [[w[8], w[7], w[6]], [w[5], w[4], w[3]], [w[2], w[1], w[0]]]
                    e = {}
                    for k in range(4):
                        e[k // 2, k % 2] = [
                            jnp.where(
                                keep[q],
                                e_s[pl.ds(r, 8), SLAB * k + 128 * q : SLAB * k + 128 * (q + 1)] + w[9],
                                0.0,
                            )
                            for q in range(2)
                        ]
                    views = side_views(e)
                    d = conv(views, taps, w[10], low, high)
                    dd, us = {}, []
                    for k in range(4):
                        out = []
                        for q in range(2):
                            value, slope = gelu_parts(d[k // 2, k % 2][q])
                            us.append(value)
                            out.append(
                                du_s[pl.ds(r, 8), SLAB * k + 128 * q : SLAB * k + 128 * (q + 1)] * slope
                            )
                        dd[k // 2, k % 2] = out
                    u_parts.append(us)
                    gsum = None
                    for k in range(4):
                        for q in range(2):
                            v = dd[k // 2, k % 2][q]
                            gsum = v if gsum is None else gsum + v
                    gh[10, pl.ds(chan, 8), :] += gsum
                    sums = tap_grads(views, dd, low, high)
                    for k in range(9):
                        gh[k, pl.ds(chan, 8), :] += sums[k // 3][k % 3]
                    de = conv(side_views(dd), flipped, None, low, high)
                    des = [
                        jnp.where(keep[q], de[k // 2, k % 2][q], 0.0) for k in range(4) for q in range(2)
                    ]
                    de_parts.append(des)
                esums = [None, None]
                for k in range(8):
                    ls = slice(128 * k, 128 * (k + 1))
                    u_s[pl.ds(row, 16), ls] = jnp.concatenate(
                        [u_parts[0][k], u_parts[1][k]], 0
                    ).astype(BF16)
                    de16 = jnp.concatenate([de_parts[0][k], de_parts[1][k]], 0).astype(BF16)
                    de_s[pl.ds(row, 16), ls] = de16
                    wide = de16.astype(F32)
                    for half in range(2):
                        v = wide[8 * half : 8 * half + 8]
                        esums[half] = v if esums[half] is None else esums[half] + v
                chan = aligned(BLK * c + row, 16)
                gh[9, pl.ds(chan, 8), :] += esums[0]
                gh[9, pl.ds(aligned(chan + 8, 8), 8), :] += esums[1]
                return carry

            lax.fori_loop(0, BLK // 16, group, 0)
            acc[...] += dot_nn(wdt[c], u_s[...])
            dgt[...] += dot_nn(wu[c], de_s[...])
            gwd[c] += dot_nt(u_s[...], dzt[...])
            gwu[c] += dot_nt(gt[...], de_s[...])
            return carry

        lax.fori_loop(0, NBLK, block, 0)
        dbt[...] = acc[...].astype(BF16)
        give(dbt, out_ref)

        def middle(row, parts):
            for half in range(2):
                r = aligned(row + 8 * half, 8)
                z = dzt[pl.ds(row, 16), :].astype(F32)[8 * half : 8 * half + 8]
                gv[V_DB, pl.ds(r, 8), :] += fold(z)
                parts[half] = parts[half] + z
            both = jnp.concatenate(parts, 0)
            acc[pl.ds(row, 16), :] = both
            low_part = both.astype(BF16)
            dbt[pl.ds(row, 16), :] = low_part
            wide = low_part.astype(F32)
            for half in range(2):
                r = aligned(row + 8 * half, 8)
                gv[V_OB, pl.ds(r, 8), :] += fold(wide[8 * half : 8 * half + 8])

        norm_back(dgt, yt, stat[2], stat[3], vt, V_MG, gv, V_MG, V_MB, middle)
        dmt[...] = dot_nn(wo[...], dbt[...]).astype(BF16)
        gwo[...] += dot_nt(mt[...], dbt[...])

        def head_backward(h, carry):
            r = aligned(HEADSZ * h, HEADSZ)
            hs = pl.ds(r, HEADSZ)
            da = e_s.at[pl.ds(0, KEYC), :]
            da[...] = dot_nn(vc[h], dmt[hs, :])

            def tile(t, carry):
                ls = pl.ds(aligned(128 * t, 128), 128)
                p = att[h, :, ls]
                g = da[:, ls]
                total = jnp.sum(p * g, 0, keepdims=True)
                dsb[:, ls] = (p * (g - total)).astype(BF16)
                return carry

            lax.fori_loop(0, TOK // 128, tile, 0)
            dkvc[pl.ds(aligned(C + r, HEADSZ), HEADSZ), :] = dot_nt(dmt[hs, :], attb[h]).astype(BF16)
            dqt[hs, :] = (dot_nn(kvc[hs, :], dsb[...]) * HEADSZ**-0.5).astype(BF16)
            dkvc[hs, :] = (dot_nt(qt[hs, :], dsb[...]) * HEADSZ**-0.5).astype(BF16)
            return carry

        lax.fori_loop(0, HEADS, head_backward, 0)
        kvt[...] = dot_nn(dkvc[...], sel[...]).astype(BF16)
        gwkv[...] += dot_nt(nt[...], kvt[...])
        dnt = dgt.at[:, pl.ds(0, SLAB)]
        dnt[...] = dot_nn(wkv[...], kvt[...])

        def vbias(i, carry):
            row = aligned(16 * i, 16)
            wide = kvt[pl.ds(aligned(C + row, 16), 16), :].astype(F32)
            gv[V_VB, pl.ds(row, 16), :] += fold(wide)
            return carry

        lax.fori_loop(0, C // 16, vbias, 0)

        def keys_out(row, parts):
            low_part = jnp.concatenate(parts, 0).astype(BF16)
            nt[pl.ds(row, 16), :] = low_part
            gv[V_RB, pl.ds(row, 16), :] += fold(low_part.astype(F32))

        norm_back(
            dnt, rt, stat[4, :, :SLAB], stat[5, :, :SLAB], vt, V_KG, gv, V_KG, V_KB, keys_out
        )
        for k in range(4):
            ls = slice(SLAB * k, SLAB * (k + 1))
            gwr[k] += dot_nt(ht_[:, ls], nt[...])
            dgt[:, ls] = dot_nn(wq[...], dqt[:, ls]) + dot_nn(wr[k], nt[...])
        gwq[...] += dot_nt(ht_[...], dqt[...])

        def qbias(i, carry):
            row = aligned(16 * i, 16)
            gv[V_QB, pl.ds(row, 16), :] += fold(dqt[pl.ds(row, 16), :].astype(F32))
            return carry

        lax.fori_loop(0, C // 16, qbias, 0)

        def final(row, parts):
            both = jnp.concatenate(parts, 0) + acc[pl.ds(row, 16), :]
            dbt[pl.ds(row, 16), :] = both.astype(BF16)

        norm_back(dgt, xt, stat[0], stat[1], vt, V_NG, gv, V_NG, V_NB, final)
        give(dbt, gin_ref)

    @pl.when(slot == pl.num_programs(0) - 1)
    def _():
        pairs = (
            (gwq, gwq_o), (gwr, gwr_o), (gwkv, gwkv_o), (gwo, gwo_o),
            (gwu, gwu_o), (gwd, gwd_o), (gv, gv_o), (gh, gh_o),
        )
        copies = [pltpu.make_async_copy(a, b, sem.at[k]) for k, (a, b) in enumerate(pairs)]
        for cp in copies:
            cp.start()
        for cp in copies:
            cp.wait()


def run_images(live, images, cotangent, weights):
    slots = images.shape[0]
    item = pl.BlockSpec((1, NTOK, C), lambda s, n: (jnp.minimum(s, n[0] - 1), 0, 0))
    out_item = pl.BlockSpec((1, NTOK, C), lambda s, n: (s, 0, 0))

    def fixed(array):
        dims = array.shape
        return pl.BlockSpec(dims, lambda s, n: (0,) * len(dims), pipeline_mode=pl.Buffered(1))

    anywhere = pl.BlockSpec(memory_space=pl.ANY)
    grads = [
        (C, C), (4, C, C), (C, 2 * C), (C, C), (NBLK, C, BLK), (NBLK, BLK, C),
        (11, C, 128), (11, HID, 128),
    ]
    wide = lambda *dims: pltpu.VMEM(dims, F32)
    thin = lambda *dims: pltpu.VMEM(dims, BF16)
    scratch = [wide(*dims) for dims in grads] + [
        thin(C, C), thin(KEYC, SLAB), wide(3, NTOK, 128), wide(TOK, 384),
        wide(C, TOK), thin(C, TOK), thin(2, C, TOK), thin(C, TOK),
        wide(HEADS, KEYC, TOK), thin(HEADS, KEYC, TOK), thin(C, TOK), wide(C, TOK),
        wide(C, TOK), wide(C, TOK), thin(C, TOK), thin(C, TOK), thin(C, TOK),
        wide(C, SLAB), thin(C, SLAB), thin(2 * C, SLAB), thin(2 * C, KEYC),
        thin(HEADS, KEYC, HEADSZ), thin(HEADS, KEYC, HEADSZ), thin(KEYC, TOK), thin(2 * C, KEYC),
        wide(BLK, TOK), wide(BLK, TOK), thin(BLK, TOK), thin(BLK, TOK), wide(6, 8, TOK),
        pltpu.SemaphoreType.DMA((len(grads),)),
    ]
    call = pl.pallas_call(
        image_kernel,
        out_shape=[jax.ShapeDtypeStruct(images.shape, BF16)] * 2
        + [jax.ShapeDtypeStruct(dims, F32) for dims in grads],
        grid_spec=pltpu.PrefetchScalarGridSpec(
            num_scalar_prefetch=1,
            grid=(slots,),
            in_specs=[item, item] + [fixed(w) for w in weights],
            out_specs=[out_item, out_item] + [anywhere] * len(grads),
            scratch_shapes=scratch,
        ),
        compiler_params=pltpu.CompilerParams(
            dimension_semantics=("arbitrary",), vmem_limit_bytes=67043328
        ),
        name="image_block",
    )
    return call(live, images, cotangent, *weights)


def prepare(p):
    wq, wo, wkv = p["query_weight"], p["out_weight"], p["kv_weight"]
    wr = p["reduce_weight"].reshape(4, C, C)
    wu = p["up_weight"].reshape(C, NBLK, BLK).transpose(1, 0, 2)
    wd = p["down_weight"].reshape(NBLK, BLK, C)
    flip = lambda w: jnp.swapaxes(w, -1, -2)
    names = (
        "norm_gain", "norm_bias", "query_bias", "reduce_bias", "keys_gain", "keys_bias",
        "value_bias", "out_bias", "mlp_gain", "mlp_bias", "down_bias",
    )
    vt = jnp.stack([p[n] for n in names], 1).astype(F32)
    ht = jnp.concatenate([p["depth_weight"], p["up_bias"][None], p["depth_bias"][None]], 0).T
    vt = jnp.pad(vt, ((0, 0), (0, 128 - 11)))
    ht = jnp.pad(ht.astype(F32), ((0, 0), (0, 128 - 11)))
    return [
        flip(wq), flip(wr), flip(wkv), flip(wo), flip(wu), flip(wd),
        wq, wr, wkv, wo, wu, wd, vt, ht,
    ]


def collect(gwq, gwr, gwkv, gwo, gwu, gwd, gv, gh):
    v = jnp.sum(gv, -1)
    h = jnp.sum(gh, -1)
    return {
        "norm_gain": v[V_NG], "norm_bias": v[V_NB], "query_weight": gwq, "query_bias": v[V_QB],
        "reduce_weight": gwr, "reduce_bias": v[V_RB], "keys_gain": v[V_KG], "keys_bias": v[V_KB],
        "kv_weight": gwkv, "value_bias": v[V_VB], "out_weight": gwo, "out_bias": v[V_OB],
        "mlp_gain": v[V_MG], "mlp_bias": v[V_MB], "up_weight": gwu.transpose(1, 0, 2),
        "up_bias": h[9], "depth_weight": h[:9], "depth_bias": h[10], "down_weight": gwd,
        "down_bias": v[V_DB],
    }


def body(images, counts, cotangent, master, first_moment, second_moment, average):
    shard_low = master.astype(jnp.bfloat16)
    pieces = unpack(lax.all_gather(shard_low, ("dp", "fsdp"), axis=0, tiled=True))
    results = run_images(counts, images, cotangent, prepare(pieces))
    output_images, grad_images = results[:2]
    terms = collect(*results[2:])
    flat_grads = jnp.concatenate([terms[n].reshape(-1) for n, _ in segments()])
    full_length = master.shape[0] * lax.axis_size("dp") * lax.axis_size("fsdp")
    flat_grads = jnp.pad(flat_grads, (0, full_length - flat_grads.shape[0]))
    grads = lax.psum_scatter(flat_grads, ("dp", "fsdp"), scatter_dimension=0, tiled=True)
    new_first = beta_first * first_moment + (1.0 - beta_first) * grads
    new_second = beta_second * second_moment + (1.0 - beta_second) * grads * grads
    fix_first = 1.0 - beta_first**STEP
    fix_second = 1.0 - beta_second**STEP
    step_size = (
        new_first / fix_first / (jnp.sqrt(new_second / fix_second) + adam_eps)
        + weight_decay * master
    )
    new_master = master - learn_rate * step_size
    new_average = ema_keep * average + (1.0 - ema_keep) * new_master
    return (
        grads,
        new_first,
        new_second,
        new_master,
        new_average,
        new_master.astype(jnp.bfloat16),
        output_images,
        grad_images,
    )


def solution(mesh):
    return jax.shard_map(
        body,
        mesh=mesh,
        in_specs=(
            P(("dp", "fsdp"), None, None),
            P(("dp", "fsdp")),
            P(("dp", "fsdp"), None, None),
            P(("dp", "fsdp")),
            P(("dp", "fsdp")),
            P(("dp", "fsdp")),
            P(("dp", "fsdp")),
        ),
        out_specs=(
            P(("dp", "fsdp")),
            P(("dp", "fsdp")),
            P(("dp", "fsdp")),
            P(("dp", "fsdp")),
            P(("dp", "fsdp")),
            P(("dp", "fsdp")),
            P(("dp", "fsdp"), None, None),
            P(("dp", "fsdp"), None, None),
        ),
        check_vma=False,
    )
```

profile of v0, /device:TPU:0, one launch (start us, length us, event | category | flops | bytes accessed | tf_op | source)
XLA Modules:
  0.0 903.0 jit_solution(3617197079689807124)
XLA Ops:
  7.2 0.9 convert_element_type.17
  9.0 6.2 copy.56.x_ref
  15.3 3.7 copy.57.ct_ref
  19.6 65.2 %all-gather.3.cloned.1.call-done = bf16[32,1,51840]{2,1,0:T(2,128)(2,1)} async-done(((bf16[1,1,51840]{2,1,0:T(2,128)(2,1)}), bf16[32,1,51840]{2,1,0:T(2,128)(2,1)}) %all-gather.3.cloned.1.call-update) | async-done | bytes 3317776 | tf_op jit(solution)/shard_map/all_gather | solution.py:630
  84.8 21.5 %reduce = bf16[32,51840]{1,0:T(8,128)(2,1)} reduce(bf16[32,1,51840]{2,1,0:T(2,128)(2,1)} %all-gather.3.cloned.1.call-done, bf16[]{:T(256)} %constant.34), dimensions={1}, to_apply=%all-gather.reduce_sub_computation | reduce | bytes 6635522 | tf_op jit(solution)/shard_map/all_gather | solution.py:630
  106.3 6.2 reshape.82
  113.3 1.9 fusion.5
  115.2 2.3 reshape_reshape.10
  117.5 2.5 copy.51
  120.0 2.4 copy.66
  125.6 0.9 pad_convert_fusion.ht
  126.5 2.0 reshape_reshape.9.wr
  128.6 1.4 copy.59.wrt
  130.8 0.9 copy-done
  131.8 1.3 copy.52
  137.1 1.0 copy.60.wkvt
  138.1 180.4 %image_block.1 = (bf16[6,784,320]{2,1,0:T(8,128)(2,1)}, bf16[6,784,320]{2,1,0:T(8,128)(2,1)}, f32[320,320]{1,0:T(8,128)}, f32[4,320,320]{2,1,0:T(8,128)}, f32[32...) custom-call(s32[1]{0:T(128)S(6)} %copy.68.n_ref, ...), custom_call_target="tpu_custom_call" | custom-call | tf_op jit(solution)/shard_map/image_block/pallas_call | solution.py:592
  318.4 2.4 copy.62
  320.9 1.5 reshape.78
  322.4 2.3 reshape.75
  324.7 2.3 reshape.80
  327.1 2.1 reshape.76
  329.2 2.0 reshape.74
  331.2 2.1 reshape.77
  333.3 5.0 reduce_sum.19
  338.3 2.1 reduce_sum.18
  340.5 58.9 %concatenate.7 = f32[1656000]{0:T(1024)} concatenate(f32[320]{0:T(512)S(1)} %get-tuple-element.64, f32[320]{0:T(512)S(1)} %get-tuple-element.63, f32[102400]{0:T(1024)} %reshape.74, f32[320]{0:T(512)S(1)} %get-tuple-element.62, f32[409600]{0:T(1024)S(1)} %reshape.75, f32[320]{0:T(512)S(1)} %get-tuple-element.61, f32[320]{0:T(512)S(1)} %get-tuple-element.60, ...), dimensions={0} | concatenate | bytes 13248000 | tf_op jit(solution)/shard_map/concatenate | solution.py:634
  399.4 5.1 pad.20
  404.5 6.1 copy.63
  410.6 6.1 copy.64
  416.7 476.7 %all-reduce.6.cloned.1.call-done = f32[1658880]{0:T(1024)} async-done(((f32[1658880]{0:T(1024)}), f32[1658880]{0:T(1024)}) %all-reduce.6.cloned.1.call-update) | async-done | bytes 6635536
  893.4 1.9 fusion.1
  (88 shorter events, 10.4 us)
Async XLA Ops:
  7.2 77.7 %all-gather.3.cloned.1.call-start = ((), (), s32[]{:S(2)}) async-start(), calls=%async_computation | async-start | bytes 6842880 | tf_op jit(solution)/shard_map/all_gather | solution.py:630
  9.0 6.3 copy-start.3
  9.0 884.4 %all-reduce.6.cloned.1.call-start = ((), (), s32[]{:S(2)}) async-start(), calls=%async_computation.1 | async-start | bytes 13271040
  119.9 4.2 copy-start.24
  119.9 4.2 copy-start.23
  119.9 4.2 copy-start.22
  119.9 4.3 copy-start.21
  119.9 4.3 copy-start.20
  119.9 4.3 copy-start.19
  120.0 4.3 copy-start.18
  120.0 4.3 copy-start.17
  120.0 4.3 copy-start.16
  120.0 4.3 copy-start.15
  120.0 4.3 copy-start.14
  124.1 5.8 copy-start.4
  126.5 6.5 copy-start.10
  128.5 1.4 copy-start.1
  128.6 7.5 copy-start.7
  130.8 1.0 copy-start
  133.3 1.1 copy-start.5
  134.4 0.7 copy-start.6
  136.3 0.8 copy-start.2
  410.6 482.8 %copy-start.9 = (f32[51840]{0:T(1024)S(1)}, f32[51840]{0:T(1024)}, u32[]{:S(2)}) copy-start(f32[51840]{0:T(1024)} %param.10) | copy-start | bytes 622084
  410.6 482.8 %copy-start.11 = (f32[51840]{0:T(1024)S(1)}, f32[51840]{0:T(1024)}, u32[]{:S(2)}) copy-start(f32[51840]{0:T(1024)} %param.12) | copy-start | bytes 622084
  410.6 482.8 %copy-start.12 = (f32[51840]{0:T(1024)S(1)}, f32[51840]{0:T(1024)}, u32[]{:S(2)}) copy-start(f32[51840]{0:T(1024)} %param.11) | copy-start | bytes 622084
  410.6 484.8 %copy-start.13 = (f32[51840]{0:T(1024)S(1)}, f32[51840]{0:T(1024)}, u32[]{:S(2)}) copy-start(f32[51840]{0:T(1024)} %param.13) | copy-start | bytes 622084
  895.4 0.8 copy-start.8
Sparse Core Ops, SparseCore 0:
  11.5 73.3 all-gather.2
  404.7 488.7 all-reduce.5
where the time goes:
time: 906 us; the launch traced here: 903 us
  waiting for transfers between devices  542 us (60%)
  Pallas kernels  180 us (20%)
  local copies, waits for them, and re-layouts  132 us (15%)
  other arithmetic  33.8 us (4%)
  between operations  15.1 us (2%)
    unnamed x3, waiting for transfers between devices  477 us
    pallas_call x1, Pallas kernels, run_images(): return call(live, images, cotangent, *weights)  180 us
    all_gather x1, waiting for transfers between devices, body(): lax.all_gather(shard_low, ('dp', 'fsdp'), axis=0, tiled=True)  65.2 us
    concatenate x1, local copies, waits for them, and re-layouts, body(): flat_grads = jnp.concatenate([terms[n].reshape(-1) for n, _ in segments()])  58.9 us
    unnamed x56, local copies, waits for them, and re-layouts  31.6 us
    all_gather x1, other arithmetic, body(): lax.all_gather(shard_low, ('dp', 'fsdp'), axis=0, tiled=True)  21.5 us
  transfers between devices with their start and end apart: 2, of which 2 were waited for; matrix products, arithmetic and copies ran while one was open for 2% of the time, Pallas kernels for 0%

commit v1 on v0

--- a/solution.py
+++ b/solution.py
@@ -1,3 +1,4 @@
+import functools
 import math
 
 import jax
@@ -25,41 +26,6 @@
 beta_first = 0.5
 beta_second = 0.5
 ema_keep = 0.9
-
-
-def segments():
-    return [
-        ("norm_gain", (C,)),
-        ("norm_bias", (C,)),
-        ("query_weight", (C, C)),
-        ("query_bias", (C,)),
-        ("reduce_weight", (4 * C, C)),
-        ("reduce_bias", (C,)),
-        ("keys_gain", (C,)),
-        ("keys_bias", (C,)),
-        ("kv_weight", (C, 2 * C)),
-        ("value_bias", (C,)),
-        ("out_weight", (C, C)),
-        ("out_bias", (C,)),
-        ("mlp_gain", (C,)),
-        ("mlp_bias", (C,)),
-        ("up_weight", (C, HID)),
-        ("up_bias", (HID,)),
-        ("depth_weight", (9, HID)),
-        ("depth_bias", (HID,)),
-        ("down_weight", (HID, C)),
-        ("down_bias", (C,)),
-    ]
-
-
-def unpack(flat_vector):
-    pieces = {}
-    offset = 0
-    for seg_name, seg_shape in segments():
-        seg_size = math.prod(seg_shape)
-        pieces[seg_name] = flat_vector[offset : offset + seg_size].reshape(seg_shape)
-        offset += seg_size
-    return pieces
 
 
 TOK = 1024
@@ -242,13 +208,175 @@
     return z * phi, phi + z * e * (1.0 / math.sqrt(2.0 * math.pi))
 
 
+ROW_QUERY, ROW_REDUCE, ROW_KEYS, ROW_KV = 0, 805, 4010, 4015
+ROW_VALUE, ROW_UP, ROW_HID, ROW_DOWN = 5615, 6425, 9625, 9735
+
+
+def rows_from_flat(flat, base, pairs, buf):
+    left = lax.broadcasted_iota(jnp.int32, (8, 128), 1) < 64
+
+    def step(i, carry):
+        t = [flat[pl.ds(base + 40 * i + k, 8, stride=5), :] for k in range(5)]
+        r = [pltpu.roll(t[k], 64, 1) for k in range(2, 5)]
+        even = (t[0], t[1], t[2])
+        odd = (jnp.where(left, r[0], r[1]), jnp.where(left, r[1], r[2]), r[2])
+        for k in range(3):
+            buf.at[k][pl.ds(16 * i, 8, stride=2), :] = even[k]
+            buf.at[k][pl.ds(16 * i + 1, 8, stride=2), :] = odd[k]
+        return carry
+
+    lax.fori_loop(0, -(-pairs // 8), step, 0)
+
+
+def rows_to_flat(flat, base, pairs, buf):
+    left = lax.broadcasted_iota(jnp.int32, (8, 128), 1) < 64
+
+    def emit(i, size):
+        even = [buf.at[k][pl.ds(16 * i, size, stride=2), :] for k in range(3)]
+        odd = [buf.at[k][pl.ds(16 * i + 1, size, stride=2), :] for k in range(3)]
+        r = [pltpu.roll(odd[k], 64, 1) for k in range(3)]
+        lo = left[:size]
+        t = (even[0], even[1], jnp.where(lo, even[2], r[0]),
+             jnp.where(lo, r[0], r[1]), jnp.where(lo, r[1], r[2]))
+        for k in range(5):
+            flat[pl.ds(base + 40 * i + k, size, stride=5), :] = t[k]
+
+    def step(i, carry):
+        emit(i, 8)
+        return carry
+
+    lax.fori_loop(0, pairs // 8, step, 0)
+    if pairs % 8:
+        emit(pairs // 8, pairs % 8)
+
+
+def buf_rows(buf, start, size):
+    at = slice(start, start + size)
+    return jnp.concatenate([buf[0, at], buf[1, at], buf[2, at][:, :64]], 1)
+
+
+def put_rows(buf, start, value):
+    at = slice(start, start + value.shape[0])
+    buf[0, at] = value[:, :128]
+    buf[1, at] = value[:, 128:256]
+    buf[2, at, :64] = value[:, 256:]
+
+
+def unpack_weights(
+    shard_rows, wall, flat, buf, eye,
+    wqt, wrt, wkvt, wot, wut, wdt, wq, wr, wkv, wo, wu, wd, vt, ht,
+):
+    for k in range(wall.shape[0]):
+        flat[shard_rows * k : shard_rows * (k + 1), :] = wall[k, :shard_rows].astype(F32)
+    tail = shard_rows * wall.shape[0]
+    flat[tail:, :] = jnp.zeros((flat.shape[0] - tail, 128), F32)
+    vectors = {}
+
+    def vector(slot, row):
+        vectors[slot] = [buf[t, row : row + 1, :] for t in range(3)]
+
+    def flip(w):
+        return dot_nt(eye[: w.shape[1], : w.shape[1]], w).astype(BF16)
+
+    rows_from_flat(flat, ROW_QUERY, 161, buf)
+    wq[...] = buf_rows(buf, 2, C).astype(BF16)
+    vector(V_NG, 0)
+    vector(V_NB, 1)
+    wqt[...] = flip(wq[...])
+    rows_from_flat(flat, ROW_REDUCE, 641, buf)
+    for k in range(4):
+        wr[k] = buf_rows(buf, 1 + C * k, C).astype(BF16)
+        wrt[k] = flip(wr[k])
+    vector(V_QB, 0)
+    vector(V_RB, 1281)
+    rows_from_flat(flat, ROW_KEYS, 1, buf)
+    vector(V_KG, 0)
+    vector(V_KB, 1)
+    for k in range(5):
+        cols = flat[pl.ds(ROW_KV + k, C, stride=5), :]
+        wkv[:, 128 * k : 128 * (k + 1)] = cols.astype(BF16)
+        wkvt[128 * k : 128 * (k + 1), :] = flip(wkv[:, 128 * k : 128 * (k + 1)])
+    rows_from_flat(flat, ROW_VALUE, 162, buf)
+    wo[...] = buf_rows(buf, 1, C).astype(BF16)
+    wot[...] = flip(wo[...])
+    vector(V_VB, 0)
+    vector(V_OB, 321)
+    vector(V_MG, 322)
+    vector(V_MB, 323)
+    for k in range(10):
+        cols = flat[pl.ds(ROW_UP + k, C, stride=10), :]
+        wu[:, 128 * k : 128 * (k + 1)] = cols.astype(BF16)
+        wut[128 * k : 128 * (k + 1), :] = flip(wu[:, 128 * k : 128 * (k + 1)])
+    rows_from_flat(flat, ROW_DOWN, 641, buf)
+    for k in range(5):
+        at = slice(BLK * k, BLK * (k + 1))
+        wd[at, :] = buf_rows(buf, BLK * k, BLK).astype(BF16)
+        wdt[:, at] = flip(wd[at, :])
+    vector(V_DB, 1280)
+    for t in range(3):
+        rows = jnp.concatenate([vectors[k][t] for k in range(11)] + [jnp.zeros((117, 128), F32)], 0)
+        size = min(128, C - 128 * t)
+        vt[128 * t : 128 * t + size, :] = rows.T[:size]
+    for k in range(10):
+        rows = flat[pl.ds(ROW_HID + k, 11, stride=10), :]
+        rows = jnp.concatenate([rows, jnp.zeros((117, 128), F32)], 0)
+        ht[128 * k : 128 * (k + 1), :] = rows.T
+
+
+def pack_grads(shard_rows, flat, buf, gwq, gwr, gwkv, gwo, gwu, gwd, gv, gh):
+    flat[ROW_DOWN + 3200 :, :] = jnp.zeros((flat.shape[0] - ROW_DOWN - 3200, 128), F32)
+
+    def vector(slot, row):
+        for t in range(3):
+            size = min(128, C - 128 * t)
+            part = gv[slot, 128 * t : 128 * t + size, :]
+            if size < 128:
+                part = jnp.concatenate([part, jnp.zeros((128 - size, 128), F32)], 0)
+            buf[t, row : row + 1, :] = jnp.sum(part.T, 0, keepdims=True)
+
+    put_rows(buf, 2, gwq[...])
+    vector(V_NG, 0)
+    vector(V_NB, 1)
+    rows_to_flat(flat, ROW_QUERY, 161, buf)
+    for k in range(4):
+        put_rows(buf, 1 + C * k, gwr[k])
+    vector(V_QB, 0)
+    vector(V_RB, 1281)
+    rows_to_flat(flat, ROW_REDUCE, 641, buf)
+    vector(V_KG, 0)
+    vector(V_KB, 1)
+    rows_to_flat(flat, ROW_KEYS, 1, buf)
+    for k in range(5):
+        flat[pl.ds(ROW_KV + k, C, stride=5), :] = gwkv[:, 128 * k : 128 * (k + 1)]
+    put_rows(buf, 1, gwo[...])
+    vector(V_VB, 0)
+    vector(V_OB, 321)
+    vector(V_MG, 322)
+    vector(V_MB, 323)
+    rows_to_flat(flat, ROW_VALUE, 162, buf)
+    for k in range(10):
+        flat[pl.ds(ROW_UP + k, C, stride=10), :] = gwu[:, 128 * k : 128 * (k + 1)]
+        for slot in range(11):
+            part = gh[slot, 128 * k : 128 * (k + 1), :]
+            at = ROW_HID + 10 * slot + k
+            flat[at : at + 1, :] = jnp.sum(part.T, 0, keepdims=True)
+    put_rows(buf, 0, gwd[...])
+    vector(V_DB, 1280)
+    for t in range(3):
+        buf[t, 1281:1282, :] = jnp.zeros((1, 128), F32)
+    rows_to_flat(flat, ROW_DOWN, 641, buf)
+    half = ROW_DOWN + 3202
+    flat[half : half + 1, 64:] = jnp.zeros((1, 64), F32)
+    flat[half + 1 :, :] = jnp.zeros((flat.shape[0] - half - 1, 128), F32)
+
+
 def image_kernel(
-    n_ref, x_ref, ct_ref,
+    shard_rows, n_ref, x_ref, ct_ref, wall,
+    out_ref, gin_ref, gflat,
     wqt, wrt, wkvt, wot, wut, wdt, wq, wr, wkv, wo, wu, wd, vt, ht,
-    out_ref, gin_ref, gwq_o, gwr_o, gwkv_o, gwo_o, gwu_o, gwd_o, gv_o, gh_o,
     gwq, gwr, gwkv, gwo, gwu, gwd, gv, gh,
-    eye, sel, xf, xp, xt, dzt, hgt, qt, att, attb, mt, yt, acc, dgt, dbt, dmt, dqt,
-    rt, nt, kvt, kvc, kc, vc, dsb, dkvc, e_s, du_s, u_s, de_s, stat, sem,
+    eye, sel, flat, xf, xp, xt, dzt, hgt, qt, attb, mt, yt, acc, dgt, dbt, dmt, dqt,
+    rt, nt, kvt, kvc, kc, vc, dsb, dkvc, e_s, du_s, u_s, de_s, stat, stage, sem,
 ):
     slot = pl.program_id(0)
     live = n_ref[0]
@@ -257,7 +385,7 @@
 
     @pl.when(slot == 0)
     def _():
-        for ref in (gwq, gwr, gwkv, gwo, gwu, gwd, gv, gh, xp):
+        for ref in (gwq, gwr, gwkv, gwo, gwu, gwd, gv, gh):
             ref[...] = jnp.zeros(ref.shape, ref.dtype)
         r = lax.broadcasted_iota(jnp.int32, (C, C), 0)
         c = lax.broadcasted_iota(jnp.int32, (C, C), 1)
@@ -267,6 +395,11 @@
         i, j = c >> 4, c & 15
         hit = (r == i * HALF + j) & (i < HALF) & (j < HALF)
         sel[...] = hit.astype(F32).astype(BF16)
+        unpack_weights(
+            shard_rows, wall, flat, xp, eye,
+            wqt, wrt, wkvt, wot, wut, wdt, wq, wr, wkv, wo, wu, wd, vt, ht,
+        )
+        xp[...] = jnp.zeros(xp.shape, F32)
 
     def take(src, dst):
         def widen(k, carry):
@@ -285,12 +418,13 @@
                     at = pl.ds(aligned((2 * a + b) * SLAB + 16 * i, 16), HALF)
                     for t in range(3):
                         rows = xf.at[t][pl.ds(56 * i + 28 * a + b, HALF, stride=2), :]
-                        xp[at, 128 * t : 128 * (t + 1)] = rows
+                        xp[t, at, :] = rows
             return carry
 
         lax.fori_loop(0, HALF, split, 0)
         for k in range(4):
-            part = xp[SLAB * k : SLAB * (k + 1), :C].astype(BF16)
+            ks = slice(SLAB * k, SLAB * (k + 1))
+            part = jnp.concatenate([xp[0, ks], xp[1, ks], xp[2, ks][:, :64]], 1).astype(BF16)
             dst[:, SLAB * k : SLAB * (k + 1)] = dot_nt(eye[...], part).astype(dst.dtype)
 
     def give(src, dst):
@@ -344,17 +478,20 @@
             r = aligned(HEADSZ * h, HEADSZ)
             kc[h] = dot_nt(sel[...], kvt[pl.ds(r, HEADSZ), :]).astype(BF16)
             vc[h] = dot_nt(sel[...], kvt[pl.ds(aligned(C + r, HEADSZ), HEADSZ), :]).astype(BF16)
-            att[h] = dot_nn(kc[h], qt[pl.ds(r, HEADSZ), :])
+            scores = dot_nn(kc[h], qt[pl.ds(r, HEADSZ), :])
+            for t in range(TOK // 128):
+                flat[pl.ds(aligned((h * 8 + t) * KEYC, 8), KEYC), :] = scores[:, 128 * t : 128 * (t + 1)]
 
             def tile(t, carry):
                 ls = pl.ds(aligned(128 * t, 128), 128)
-                s = att[h, :, ls]
+                at = pl.ds(aligned((h * 8 + t) * KEYC, 8), KEYC)
+                s = flat[at, :]
                 rows = lax.broadcasted_iota(jnp.int32, (KEYC, 128), 0)
                 s = jnp.where(rows < KEYS, s, -jnp.inf)
                 top = jnp.max(s, 0, keepdims=True)
                 p = jnp.exp2((s - top) * (LOG2E * HEADSZ**-0.5))
                 p = p * (1.0 / jnp.sum(p, 0, keepdims=True))
-                att[h, :, ls] = p
+                flat[at, :] = p
                 attb[h, :, ls] = p.astype(BF16)
                 return carry
 
@@ -375,8 +512,9 @@
         keep = (lane16, lane16 & (lanes < 96))
 
         def block(c, carry):
-            e_s[...] = dot_nn(wut[c], gt[...])
-            du_s[...] = dot_nn(wd[c], dzt[...])
+            span = pl.ds(aligned(BLK * c, BLK), BLK)
+            e_s[...] = dot_nn(wut[span, :], gt[...])
+            du_s[...] = dot_nn(wd[span, :], dzt[...])
 
             def group(i, carry):
                 row = aligned(16 * i, 16)
@@ -386,14 +524,14 @@
                     chan = aligned(BLK * c + r, 8)
                     table = ht[pl.ds(chan, 8), :]
                     w = [jnp.broadcast_to(table[:, k : k + 1], (8, 128)) for k in range(11)]
-                    taps = [w[0:3], w[3:6], w[6:9]]
-                    flipped = [[w[8], w[7], w[6]], [w[5], w[4], w[3]], [w[2], w[1], w[0]]]
+                    taps = [w[1:4], w[4:7], w[7:10]]
+                    flipped = [[w[9], w[8], w[7]], [w[6], w[5], w[4]], [w[3], w[2], w[1]]]
                     e = {}
                     for k in range(4):
                         e[k // 2, k % 2] = [
                             jnp.where(
                                 keep[q],
-                                e_s[pl.ds(r, 8), SLAB * k + 128 * q : SLAB * k + 128 * (q + 1)] + w[9],
+                                e_s[pl.ds(r, 8), SLAB * k + 128 * q : SLAB * k + 128 * (q + 1)] + w[0],
                                 0.0,
                             )
                             for q in range(2)
@@ -419,7 +557,7 @@
                     gh[10, pl.ds(chan, 8), :] += gsum
                     sums = tap_grads(views, dd, low, high)
                     for k in range(9):
-                        gh[k, pl.ds(chan, 8), :] += sums[k // 3][k % 3]
+                        gh[k + 1, pl.ds(chan, 8), :] += sums[k // 3][k % 3]
                     de = conv(side_views(dd), flipped, None, low, high)
                     des = [
                         jnp.where(keep[q], de[k // 2, k % 2][q], 0.0) for k in range(4) for q in range(2)
@@ -438,15 +576,15 @@
                         v = wide[8 * half : 8 * half + 8]
                         esums[half] = v if esums[half] is None else esums[half] + v
                 chan = aligned(BLK * c + row, 16)
-                gh[9, pl.ds(chan, 8), :] += esums[0]
-                gh[9, pl.ds(aligned(chan + 8, 8), 8), :] += esums[1]
+                gh[0, pl.ds(chan, 8), :] += esums[0]
+                gh[0, pl.ds(aligned(chan + 8, 8), 8), :] += esums[1]
                 return carry
 
             lax.fori_loop(0, BLK // 16, group, 0)
-            acc[...] += dot_nn(wdt[c], u_s[...])
-            dgt[...] += dot_nn(wu[c], de_s[...])
-            gwd[c] += dot_nt(u_s[...], dzt[...])
-            gwu[c] += dot_nt(gt[...], de_s[...])
+            acc[...] += dot_nn(wdt[:, span], u_s[...])
+            dgt[...] += dot_nn(wu[:, span], de_s[...])
+            gwd[span, :] += dot_nt(u_s[...], dzt[...])
+            gwu[:, span] += dot_nt(gt[...], de_s[...])
             return carry
 
         lax.fori_loop(0, NBLK, block, 0)
@@ -480,7 +618,7 @@
 
             def tile(t, carry):
                 ls = pl.ds(aligned(128 * t, 128), 128)
-                p = att[h, :, ls]
+                p = flat[pl.ds(aligned((h * 8 + t) * KEYC, 8), KEYC), :]
                 g = da[:, ls]
                 total = jnp.sum(p * g, 0, keepdims=True)
                 dsb[:, ls] = (p * (g - total)).astype(BF16)
@@ -536,52 +674,56 @@
 
     @pl.when(slot == pl.num_programs(0) - 1)
     def _():
-        pairs = (
-            (gwq, gwq_o), (gwr, gwr_o), (gwkv, gwkv_o), (gwo, gwo_o),
-            (gwu, gwu_o), (gwd, gwd_o), (gv, gv_o), (gh, gh_o),
-        )
-        copies = [pltpu.make_async_copy(a, b, sem.at[k]) for k, (a, b) in enumerate(pairs)]
-        for cp in copies:
-            cp.start()
-        for cp in copies:
-            cp.wait()
-
-
-def run_images(live, images, cotangent, weights):
+        pack_grads(shard_rows, flat, xp, gwq, gwr, gwkv, gwo, gwu, gwd, gv, gh)
+        copies = []
+        for k in range(gflat.shape[0]):
+            if k >= 2:
+                copies[k - 2].wait()
+            stage[k % 2] = flat[shard_rows * k : shard_rows * k + gflat.shape[1], :]
+            copies.append(pltpu.make_async_copy(stage.at[k % 2], gflat.at[k], sem.at[k % 2]))
+            copies[k].start()
+        copies[-2].wait()
+        copies[-1].wait()
+
+
+def run_images(live, images, cotangent, gathered, shard_rows):
     slots = images.shape[0]
+    count, padded = gathered.shape[:2]
     item = pl.BlockSpec((1, NTOK, C), lambda s, n: (jnp.minimum(s, n[0] - 1), 0, 0))
     out_item = pl.BlockSpec((1, NTOK, C), lambda s, n: (s, 0, 0))
-
-    def fixed(array):
-        dims = array.shape
-        return pl.BlockSpec(dims, lambda s, n: (0,) * len(dims), pipeline_mode=pl.Buffered(1))
-
     anywhere = pl.BlockSpec(memory_space=pl.ANY)
-    grads = [
-        (C, C), (4, C, C), (C, 2 * C), (C, C), (NBLK, C, BLK), (NBLK, BLK, C),
-        (11, C, 128), (11, HID, 128),
-    ]
     wide = lambda *dims: pltpu.VMEM(dims, F32)
     thin = lambda *dims: pltpu.VMEM(dims, BF16)
-    scratch = [wide(*dims) for dims in grads] + [
-        thin(C, C), thin(KEYC, SLAB), wide(3, NTOK, 128), wide(TOK, 384),
+    flat_rows = -(-(count * shard_rows + 24) // 8) * 8
+    scratch = [
+        thin(C, C), thin(4, C, C), thin(2 * C, C), thin(C, C), thin(HID, C), thin(C, HID),
+        thin(C, C), thin(4, C, C), thin(C, 2 * C), thin(C, C), thin(C, HID), thin(HID, C),
+        wide(C, 128), wide(HID, 128),
+        wide(C, C), wide(4, C, C), wide(C, 2 * C), wide(C, C), wide(C, HID), wide(HID, C),
+        wide(11, C, 128), wide(11, HID, 128),
+        thin(C, C), thin(KEYC, SLAB), wide(flat_rows, 128), wide(3, NTOK, 128), wide(3, 1296, 128),
         wide(C, TOK), thin(C, TOK), thin(2, C, TOK), thin(C, TOK),
-        wide(HEADS, KEYC, TOK), thin(HEADS, KEYC, TOK), thin(C, TOK), wide(C, TOK),
+        thin(HEADS, KEYC, TOK), thin(C, TOK), wide(C, TOK),
         wide(C, TOK), wide(C, TOK), thin(C, TOK), thin(C, TOK), thin(C, TOK),
         wide(C, SLAB), thin(C, SLAB), thin(2 * C, SLAB), thin(2 * C, KEYC),
         thin(HEADS, KEYC, HEADSZ), thin(HEADS, KEYC, HEADSZ), thin(KEYC, TOK), thin(2 * C, KEYC),
         wide(BLK, TOK), wide(BLK, TOK), thin(BLK, TOK), thin(BLK, TOK), wide(6, 8, TOK),
-        pltpu.SemaphoreType.DMA((len(grads),)),
+        wide(2, padded, 128), pltpu.SemaphoreType.DMA((2,)),
     ]
     call = pl.pallas_call(
-        image_kernel,
+        functools.partial(image_kernel, shard_rows),
         out_shape=[jax.ShapeDtypeStruct(images.shape, BF16)] * 2
-        + [jax.ShapeDtypeStruct(dims, F32) for dims in grads],
+        + [jax.ShapeDtypeStruct((count, padded, 128), F32)],
         grid_spec=pltpu.PrefetchScalarGridSpec(
             num_scalar_prefetch=1,
             grid=(slots,),
-            in_specs=[item, item] + [fixed(w) for w in weights],
-            out_specs=[out_item, out_item] + [anywhere] * len(grads),
+            in_specs=[
+                item, item,
+                pl.BlockSpec(
+                    gathered.shape, lambda s, n: (0, 0, 0), pipeline_mode=pl.Buffered(1)
+                ),
+            ],
+            out_specs=[out_item, out_item, anywhere],
             scratch_shapes=scratch,
         ),
         compiler_params=pltpu.CompilerParams(
@@ -589,52 +731,213 @@
         ),
         name="image_block",
     )
-    return call(live, images, cotangent, *weights)
-
-
-def prepare(p):
-    wq, wo, wkv = p["query_weight"], p["out_weight"], p["kv_weight"]
-    wr = p["reduce_weight"].reshape(4, C, C)
-    wu = p["up_weight"].reshape(C, NBLK, BLK).transpose(1, 0, 2)
-    wd = p["down_weight"].reshape(NBLK, BLK, C)
-    flip = lambda w: jnp.swapaxes(w, -1, -2)
-    names = (
-        "norm_gain", "norm_bias", "query_bias", "reduce_bias", "keys_gain", "keys_bias",
-        "value_bias", "out_bias", "mlp_gain", "mlp_bias", "down_bias",
+    return call(live, images, cotangent, gathered)
+
+
+MESH = pl.DeviceIdType.MESH
+
+
+class Place:
+    def __init__(self, dims):
+        self.dp, self.fsdp = dims
+        self.ny, self.nz = self.dp // 2, self.fsdp // 2
+        dp, fsdp = lax.axis_index("dp"), lax.axis_index("fsdp")
+        self.y, self.c = dp // 2, dp % 2
+        self.z, self.x = fsdp // 2, fsdp % 2
+        self.offsets = [(dy, dx) for dy in range(self.ny) for dx in range(2)]
+
+    def at(self, dy=0, dc=0, dz=0, dx=0):
+        y, c = (self.y + dy) % self.ny, (self.c + dc) % 2
+        z, x = (self.z + dz) % self.nz, (self.x + dx) % 2
+        return y * 2 + c, z * 2 + x
+
+    def index(self, **move):
+        dp, fsdp = self.at(**move)
+        return dp * self.fsdp + fsdp
+
+    def target(self, **move):
+        dp, fsdp = self.at(**move)
+        return {"dp": dp, "fsdp": fsdp}
+
+    def peers(self):
+        moves = [dict(dz=k) for k in range(1, self.nz)]
+        moves += [dict(dy=dy, dx=dx) for dy, dx in self.offsets[1:]]
+        return moves + [dict(dc=1)]
+
+    def enter(self):
+        barrier = pltpu.get_barrier_semaphore()
+        moves = self.peers()
+        for move in moves:
+            pl.semaphore_signal(barrier, inc=1, device_id=self.target(**move), device_id_type=MESH)
+        pl.semaphore_wait(barrier, len(moves))
+
+
+def remote(src, dst, send, recv, target):
+    return pltpu.make_async_remote_copy(
+        src_ref=src, dst_ref=dst, send_sem=send, recv_sem=recv, device_id=target, device_id_type=MESH
     )
-    vt = jnp.stack([p[n] for n in names], 1).astype(F32)
-    ht = jnp.concatenate([p["depth_weight"], p["up_bias"][None], p["depth_bias"][None]], 0).T
-    vt = jnp.pad(vt, ((0, 0), (0, 128 - 11)))
-    ht = jnp.pad(ht.astype(F32), ((0, 0), (0, 128 - 11)))
-    return [
-        flip(wq), flip(wr), flip(wkv), flip(wo), flip(wu), flip(wd),
-        wq, wr, wkv, wo, wu, wd, vt, ht,
-    ]
-
-
-def collect(gwq, gwr, gwkv, gwo, gwu, gwd, gv, gh):
-    v = jnp.sum(gv, -1)
-    h = jnp.sum(gh, -1)
-    return {
-        "norm_gain": v[V_NG], "norm_bias": v[V_NB], "query_weight": gwq, "query_bias": v[V_QB],
-        "reduce_weight": gwr, "reduce_bias": v[V_RB], "keys_gain": v[V_KG], "keys_bias": v[V_KB],
-        "kv_weight": gwkv, "value_bias": v[V_VB], "out_weight": gwo, "out_bias": v[V_OB],
-        "mlp_gain": v[V_MG], "mlp_bias": v[V_MB], "up_weight": gwu.transpose(1, 0, 2),
-        "up_bias": h[9], "depth_weight": h[:9], "depth_bias": h[10], "down_weight": gwd,
-        "down_bias": v[V_DB],
-    }
+
+
+def gather_kernel(dims, low_ref, out_ref, send, recv):
+    p = Place(dims)
+    p.enter()
+    started = []
+
+    def push(src, slot, **move):
+        cp = remote(src, out_ref.at[slot], send.at[len(started)], recv.at[slot], p.target(**move))
+        cp.start()
+        started.append(cp)
+
+    def arrived(slot):
+        remote(low_ref, out_ref.at[slot], send.at[0], recv.at[slot], p.target(dc=1)).wait_recv()
+
+    mine = p.index()
+    for dz in range(1, p.nz):
+        push(low_ref, mine, dz=dz)
+    out_ref[mine] = low_ref[...]
+    for dz in range(p.nz):
+        slot = p.index(dz=dz)
+        if dz:
+            arrived(slot)
+        src = out_ref.at[slot] if dz else low_ref
+        for dy, dx in p.offsets[1:]:
+            push(src, slot, dy=dy, dx=dx)
+        push(src, slot, dc=1)
+    for dz in range(p.nz):
+        for dy, dx in p.offsets[1:]:
+            slot = p.index(dz=dz, dy=dy, dx=dx)
+            arrived(slot)
+            push(out_ref.at[slot], slot, dc=1)
+    for dz in range(p.nz):
+        for dy, dx in p.offsets:
+            arrived(p.index(dz=dz, dy=dy, dx=dx, dc=1))
+    for cp in started:
+        cp.wait_send()
+
+
+def all_weights(dims, low):
+    count = dims[0] * dims[1]
+    ny, nz = dims[0] // 2, dims[1] // 2
+    sends = nz - 1 + nz * 2 * ny + nz * (2 * ny - 1)
+    vmem = pl.BlockSpec(memory_space=pltpu.VMEM)
+    return pl.pallas_call(
+        functools.partial(gather_kernel, dims),
+        out_shape=jax.ShapeDtypeStruct((count,) + low.shape, low.dtype),
+        in_specs=[vmem],
+        out_specs=vmem,
+        scratch_shapes=[pltpu.SemaphoreType.DMA((sends,)), pltpu.SemaphoreType.DMA((count,))],
+        compiler_params=pltpu.CompilerParams(
+            collective_id=0, has_side_effects=True, vmem_limit_bytes=32 * 1024 * 1024
+        ),
+        name="weights_gather",
+    )(low)
+
+
+def scatter_kernel(dims, g_ref, out_ref, mine, other, sx, rx, sz, rz, lsem, csem, xsem, zsem):
+    p = Place(dims)
+    p.enter()
+    n_xy = len(p.offsets)
+    order = list(range(1, p.nz)) + [0]
+    local, cross = {}, {}
+    for dz in order:
+        for k, (dy, dx) in enumerate(p.offsets):
+            cp = remote(
+                g_ref.at[p.index(dy=dy, dx=dx, dz=dz, dc=1)], other.at[dz, k],
+                csem.at[0, dz, k], csem.at[1, dz, k], p.target(dc=1),
+            )
+            cp.start()
+            cross[dz, k] = cp
+            cp = pltpu.make_async_copy(
+                g_ref.at[p.index(dy=dy, dx=dx, dz=dz)], mine.at[dz, k], lsem.at[dz, k]
+            )
+            cp.start()
+            local[dz, k] = cp
+    planar = {}
+    waiting = None
+    for dz in order:
+        for k in list(range(1, n_xy)) + [0]:
+            dy, dx = p.offsets[k]
+            local[dz, k].wait()
+            cross[dz, k].wait_recv()
+            total = mine[dz, k] + other[dz, k]
+            if k == 0:
+                mine[dz, 0] = total
+            else:
+                sx[dz, k - 1] = total.astype(BF16)
+            if waiting is not None:
+                waiting.start()
+                waiting = None
+            if k:
+                waiting = remote(
+                    sx.at[dz, k - 1], rx.at[dz, k - 1],
+                    xsem.at[0, dz, k - 1], xsem.at[1, dz, k - 1], p.target(dy=dy, dx=dx),
+                )
+                planar[dz, k] = waiting
+    final = None
+    lines = {}
+    for dz in order:
+        total = mine[dz, 0]
+        for k in range(1, n_xy):
+            planar[dz, k].wait_recv()
+            total = total + rx[dz, k - 1].astype(F32)
+        if dz:
+            sz[dz - 1] = total.astype(BF16)
+        else:
+            final = total
+        if waiting is not None:
+            waiting.start()
+            waiting = None
+        if dz:
+            waiting = remote(
+                sz.at[dz - 1], rz.at[dz - 1], zsem.at[0, dz - 1], zsem.at[1, dz - 1], p.target(dz=dz)
+            )
+            lines[dz] = waiting
+    for dz in range(1, p.nz):
+        lines[dz].wait_recv()
+        final = final + rz[dz - 1].astype(F32)
+    out_ref[...] = final
+    for group in (cross, planar, lines):
+        for cp in group.values():
+            cp.wait_send()
+
+
+def sum_to_owner(dims, terms):
+    ny, nz = dims[0] // 2, dims[1] // 2
+    n_xy = 2 * ny
+    rows = terms.shape[1]
+    dma = pltpu.SemaphoreType.DMA
+    return pl.pallas_call(
+        functools.partial(scatter_kernel, dims),
+        out_shape=jax.ShapeDtypeStruct((rows, 128), F32),
+        in_specs=[pl.BlockSpec(memory_space=pl.ANY)],
+        out_specs=pl.BlockSpec(memory_space=pltpu.VMEM),
+        scratch_shapes=[
+            pltpu.VMEM((nz, n_xy, rows, 128), F32),
+            pltpu.VMEM((nz, n_xy, rows, 128), F32),
+            pltpu.VMEM((nz, n_xy - 1, rows, 128), BF16),
+            pltpu.VMEM((nz, n_xy - 1, rows, 128), BF16),
+            pltpu.VMEM((nz - 1, rows, 128), BF16),
+            pltpu.VMEM((nz - 1, rows, 128), BF16),
+            dma((nz, n_xy)), dma((2, nz, n_xy)), dma((2, nz, n_xy - 1)), dma((2, nz - 1)),
+        ],
+        compiler_params=pltpu.CompilerParams(
+            collective_id=1, has_side_effects=True, vmem_limit_bytes=48 * 1024 * 1024
+        ),
+        name="grads_scatter",
+    )(terms)
 
 
 def body(images, counts, cotangent, master, first_moment, second_moment, average):
-    shard_low = master.astype(jnp.bfloat16)
-    pieces = unpack(lax.all_gather(shard_low, ("dp", "fsdp"), axis=0, tiled=True))
-    results = run_images(counts, images, cotangent, prepare(pieces))
-    output_images, grad_images = results[:2]
-    terms = collect(*results[2:])
-    flat_grads = jnp.concatenate([terms[n].reshape(-1) for n, _ in segments()])
-    full_length = master.shape[0] * lax.axis_size("dp") * lax.axis_size("fsdp")
-    flat_grads = jnp.pad(flat_grads, (0, full_length - flat_grads.shape[0]))
-    grads = lax.psum_scatter(flat_grads, ("dp", "fsdp"), scatter_dimension=0, tiled=True)
+    dims = (lax.axis_size("dp"), lax.axis_size("fsdp"))
+    shard_rows = master.shape[0] // 128
+    padded = -(-shard_rows // 16) * 16
+    low = master.reshape(shard_rows, 128).astype(BF16)
+    low = jnp.pad(low, ((0, padded - shard_rows), (0, 0)))
+    gathered = all_weights(dims, low)
+    output_images, grad_images, terms = run_images(
+        counts, images, cotangent, gathered, shard_rows
+    )
+    grads = sum_to_owner(dims, terms)[:shard_rows].reshape(-1)
     new_first = beta_first * first_moment + (1.0 - beta_first) * grads
     new_second = beta_second * second_moment + (1.0 - beta_second) * grads * grads
     fix_first = 1.0 - beta_first**STEP

time: 906 us -> 634 us (0.70)
  waiting for transfers between devices: 542 us -> 0 us
  Pallas kernels: 180 us -> 606 us
  local copies, waits for them, and re-layouts: 132 us -> 23.6 us
  other arithmetic: 33.8 us -> 2.76 us
  between operations: 15.1 us -> 1.54 us
    unnamed x3 -> x0, waiting for transfers between devices: 477 us -> none
    pallas_call x1 -> x3, Pallas kernels: 180 us -> 606 us  [the longest x1 300 us: run_images(): return call(live, images, cotangent, gathered)]
    all_gather x1 -> x0, waiting for transfers between devices: 65.2 us -> none  [body(): lax.all_gather(shard_low, ('dp', 'fsdp'), axis=0, tiled=True)]
    concatenate x2 -> x0, local copies, waits for them, and re-layouts: 59.1 us -> none  [the longest x1 58.9 us: body(): flat_grads = jnp.concatenate([terms[n].reshape(-1) for n, _ in segments()])]
    all_gather x1 -> x0, other arithmetic: 21.5 us -> none  [body(): lax.all_gather(shard_low, ('dp', 'fsdp'), axis=0, tiled=True)]
    reshape x10 -> x0, local copies, waits for them, and re-layouts: 12.9 us -> none  [the longest x7 12.4 us: body(): flat_grads = jnp.concatenate([terms[n].reshape(-1) for n, _ in segments()])]
    another operation x19 -> x0, local copies, waits for them, and re-layouts: 11.6 us -> none  [the longest x3 7.17 us: prepare(): wu = p['up_weight'].reshape(C, NBLK, BLK).transpose(1, 0, 2)]
    unnamed x56 -> x18, local copies, waits for them, and re-layouts: 31.6 us -> 23.6 us
  transfers between devices with their start and end apart: 2 -> 0, of which waited for: 2 -> 0; matrix products, arithmetic and copies ran while one was open for 2% -> 0% of each run, Pallas kernels for 0% -> 0%
where the time goes in v1:
time: 634 us
  Pallas kernels  606 us (96%)
  local copies, waits for them, and re-layouts  23.6 us (4%)
    pallas_call x1, Pallas kernels, run_images(): return call(live, images, cotangent, gathered)  300 us
    pallas_call x1, Pallas kernels, sum_to_owner(): pl.pallas_call(functools.partial(scatter_kernel, dims), out_shape=jax.Sha...  277 us
    pallas_call x1, Pallas kernels, all_weights(): pl.pallas_call(functools.partial(gather_kernel, dims), out_shape=jax.Shap...  30.2 us
    unnamed x18, local copies, waits for them, and re-layouts  23.6 us

profile of v1, /device:TPU:0, one launch (start us, length us, event | category | flops | bytes accessed | tf_op | source)
XLA Modules:
  0.0 634.1 jit_solution(8386334391402683284)
XLA Ops:
  0.6 0.0 copy-start.1
  1.4 1.1 convert_bitcast_fusion
  2.6 30.2 %weights_gather.1.wall = bf16[32,416,128]{2,1,0:T(8,128)(2,1)S(1)} custom-call(bf16[416,128]{1,0:T(8,128)(2,1)S(1)} %pad.4.low_ref), custom_call_target="tpu_custom_call" | custom-call | tf_op jit(solution)/shard_map/weights_gather/pallas_call | solution.py:823
  32.7 0.0 copy-start
  32.8 1.7 copy-done
  34.5 0.0 copy-done.1
  34.5 3.7 copy.15.x_ref
  38.2 6.0 copy.16.ct_ref
  44.2 299.5 %image_block.1 = (bf16[6,784,320]{2,1,0:T(8,128)(2,1)}, bf16[6,784,320]{2,1,0:T(8,128)(2,1)}, f32[32,416,128]{2,1,0:T(8,128)}) custom-call(s32[1]{0:T(128)S(6)} %copy.19.n_ref, bf16[6,784,320]{2,1,0:T(8,128)(2,1)} %copy.15.x_ref, bf16[6,784,320]{2,1,0:T(8,128)(2,1)} %copy.16.ct_ref, bf16[32,416,128]{2,1,0:T(8,128)(2,1)} %copy-done), custom_call_target="tpu_custom_call" | custom-call | tf_op jit(solution)/shard_map/image_block/pallas_call | solution.py:734
  343.7 0.0 copy-start.3
  343.7 0.0 copy-start.5
  343.8 0.0 copy-start.6
  343.8 0.0 copy-start.4
  343.8 276.5 %grads_scatter.1 = f32[416,128]{1,0:T(8,128)S(1)} custom-call(f32[32,416,128]{2,1,0:T(8,128)} %get-tuple-element.11.g_ref), custom_call_target="tpu_custom_call" | custom-call | tf_op jit(solution)/shard_map/grads_scatter/pallas_call | solution.py:909
  620.3 0.0 copy-done.3
  620.3 0.0 copy-done.5
  620.4 0.0 copy-done.6
  620.4 0.9 fusion.1
  621.3 0.0 copy-start.2
  621.3 0.0 copy-done.4
  621.3 0.7 multiply_add_fusion.1
  622.0 6.1 copy.17
  628.1 0.0 copy-done.2
  628.1 6.1 copy.18
  (1 shorter events, 0.0 us)
Async XLA Ops:
  0.6 33.9 %copy-start.1 = (bf16[6,784,320]{1,2,0:T(8,128)(2,1)S(1)}, bf16[6,784,320]{1,2,0:T(8,128)(2,1)}, u32[]{:S(2)}) copy-start(bf16[6,784,320]{1,2,0:T(8,128)(2,1)} %param.7) | copy-start | bytes 9031684
  32.7 1.8 copy-start
  343.7 276.6 %copy-start.3 = (f32[51840]{0:T(1024)S(1)}, f32[51840]{0:T(1024)}, u32[]{:S(2)}) copy-start(f32[51840]{0:T(1024)} %param.10) | copy-start | bytes 622084
  343.7 276.6 %copy-start.5 = (f32[51840]{0:T(1024)S(1)}, f32[51840]{0:T(1024)}, u32[]{:S(2)}) copy-start(f32[51840]{0:T(1024)} %param.12) | copy-start | bytes 622084
  343.8 276.6 %copy-start.6 = (f32[51840]{0:T(1024)S(1)}, f32[51840]{0:T(1024)}, u32[]{:S(2)}) copy-start(f32[51840]{0:T(1024)} %param.11) | copy-start | bytes 622084
  343.8 277.5 %copy-start.4 = (f32[51840]{0:T(1024)S(1)}, f32[51840]{0:T(1024)}, u32[]{:S(2)}) copy-start(f32[51840]{0:T(1024)} %param.13) | copy-start | bytes 622084
  621.3 6.8 %copy-start.2 = (f32[51840]{0:T(1024)}, f32[51840]{0:T(1024)S(1)}, u32[]{:S(2)}) copy-start(f32[51840]{0:T(1024)S(1)} %get-tuple-element.23) | copy-start | bytes 622084
